TPU v7x, 256 devices: a 8x8x2 block of a 8x8x16 slice. The times are simulated.
256 devices in a mesh: cfg: 2 (over z), space: 64 (over x, y), tm: 2 (over core).
Axes of the slice: x: 8, y: 8, z: 2, core: 2. Of those that a mesh axis runs over, the one named last changes fastest.
The devices are a block of a 8x8x16 slice.
Arguments:
- vectors: bfloat16 [4, 64, 6, 65536], P(('cfg', 'tm'), 'space'), parts along dimension 0, may hold values from -0.625 to 0.625
- gauge_links: bfloat16 [4, 3, 18, 65536], P(('cfg', 'tm'), None, None, 'space'), parts along dimension 0, may hold values from -3 to 3
- momenta: int32 [8, 3], replicated, may hold values from -2 to 2
- directions: int32 [3], replicated, may hold values from 0 to 2, each once
Outputs:
- elementals: float32 [64, 4, 8, 3, 128], P('space', ('cfg', 'tm')), parts along dimension 1
There are 2 independent parts, one for each index of `cfg`. A program takes and returns all parts, laid end to end along the dimension named above; an argument that names none is the same for every part. Nothing has to cross between parts.
Inputs may be any that keep to these rules, and one draw needn't show every extreme that they name: `momenta`: integer momentum components, in units of 2 pi over the lattice extent. Each of the directions 0, 1, 2 appears once.
All inputs are finite; a program needn't handle non-finite values.
Results may differ from a plain program's by a relative error of at most 0.005.
Values may be sent and summed in bfloat16 or wider, within the bound.
A program may use at most 128 MiB of HBM per device.

v0:
```python
import functools
import math

import jax
import jax.numpy as jnp
from jax import lax
from jax.experimental import pallas as pl
from jax.experimental.pallas import tpu as pltpu
from jax.sharding import PartitionSpec as P

LXY = 32
NMOM = 8
NDIR = 3
PLANE = LXY * LXY
LANES = 128
BLOCKS = PLANE // LANES
HALF = PLANE // 2
COMPS = 6
BLOCK_ROWS = COMPS * BLOCKS
PITCH = BLOCK_ROWS + 8
DEPTH = COMPS * PLANE
TWO_PI = 2.0 * math.pi
MESH = pl.DeviceIdType.MESH
BF16, F32 = jnp.bfloat16, jnp.float32


def roll(value, shift):
    return pltpu.roll(value, shift, value.ndim - 1)


def apply_table(table, lanes, field):
    out_re, out_im = [], []
    for row in range(3):
        acc_re = acc_im = None
        for col in range(3):
            link_re = table[3 * row + col : 3 * row + col + 1, lanes]
            link_im = table[9 + 3 * row + col : 10 + 3 * row + col, lanes]
            re = link_re * field[col] - link_im * field[3 + col]
            im = link_re * field[3 + col] + link_im * field[col]
            acc_re = re if acc_re is None else acc_re + re
            acc_im = im if acc_im is None else acc_im + im
        out_re.append(acc_re)
        out_im.append(acc_im)
    return out_re + out_im


def minus_adjoint(entries):
    real = [-entries[3 * b + a] for a in range(3) for b in range(3)]
    imag = [entries[9 + 3 * b + a] for a in range(3) for b in range(3)]
    return real + imag


def lanes_at(slot, at):
    return pl.ds(pl.multiple_of(slot * PLANE + at * LANES, LANES), LANES)


def store_packed(packed, base, first, nev, rows_at, group, at, value):
    for colour in range(3):
        re = value[colour].astype(BF16)
        im = value[3 + colour].astype(BF16)
        upper, lower = pl.ds(base + rows_at, group), pl.ds(base + nev + rows_at, group)
        packed[upper, lanes_at(first + colour, at)] = re
        packed[lower, lanes_at(first + colour, at)] = im
        packed[upper, lanes_at(first + 3 + colour, at)] = im
        packed[lower, lanes_at(first + 3 + colour, at)] = -re


def store_twisted(twisted, first, nev, rows_at, group, at, cosine, sine, field):
    for mom in range(NMOM):
        cos_row = cosine[mom : mom + 1, lanes_at(0, at)]
        sin_row = sine[mom : mom + 1, lanes_at(0, at)]
        rows = pl.ds(mom * nev + rows_at, group)
        for colour in range(3):
            vec_re, vec_im = field[colour], field[3 + colour]
            twisted[rows, lanes_at(first + colour, at)] = (
                vec_re * cos_row - vec_im * sin_row
            ).astype(BF16)
            twisted[rows, lanes_at(first + 3 + colour, at)] = (
                vec_re * sin_row + vec_im * cos_row
            ).astype(BF16)


def contract(left, right):
    return lax.dot_general(left, right, (((1,), (1,)), ((), ())), preferred_element_type=F32)


def wait_for(ref, sem):
    pltpu.make_async_copy(ref, ref, sem).wait()


def fill_phases(momenta, plane, z_length, cosine, sine):
    row = lax.broadcasted_iota(jnp.int32, (NMOM, LANES), 0)
    lane = lax.broadcasted_iota(jnp.int32, (NMOM, LANES), 1)

    def column(axis):
        value = jnp.zeros((NMOM, LANES), jnp.int32)
        for mom in range(NMOM):
            value = jnp.where(row == mom, momenta[axis, mom], value)
        return value

    mom_x, mom_y, mom_z = column(0), column(1), column(2)
    part_x = jnp.bitwise_and(mom_x * jnp.bitwise_and(lane, LXY - 1), LXY - 1).astype(F32) / LXY
    y_low = jnp.right_shift(lane, LXY.bit_length() - 1)
    for at in range(BLOCKS):
        y_coord = y_low + at * (LANES // LXY)
        part_y = jnp.bitwise_and(mom_y * y_coord, LXY - 1).astype(F32) / LXY
        beside = plane + 1 if at < BLOCKS // 2 else plane + z_length - 1
        for index, z_coord in enumerate((plane, beside)):
            part_z = jnp.bitwise_and(mom_z * z_coord, z_length - 1).astype(F32) / z_length
            theta = TWO_PI * (part_x + part_y + part_z)
            cosine[index, :, at * LANES : (at + 1) * LANES] = jnp.cos(theta)
            sine[index, :, at * LANES : (at + 1) * LANES] = jnp.sin(theta)


def pack_links(links_ref, links_out, links_z_out):
    for at in range(BLOCKS):
        lanes = slice(at * LANES, (at + 1) * LANES)
        rows = [links_ref[direction, :, lanes].astype(F32) for direction in range(NDIR)]
        for direction in range(NDIR):
            links_out[at, direction * 24 : direction * 24 + 18, :] = rows[direction].astype(BF16)
        if at >= BLOCKS // 2:
            links_z_out[at - BLOCKS // 2, 0:18, :] = rows[2].astype(BF16)


def fill_tables(links, table):
    lane = lax.broadcasted_iota(jnp.int32, (1, LANES), 1)
    x_lane = jnp.bitwise_and(lane, LXY - 1)

    def block(index):
        return slice(index * LANES, (index + 1) * LANES)

    for direction in range(2):
        for at in range(BLOCKS):
            wide = 0.5 * links[at, direction * 24 : direction * 24 + 24, :].astype(F32)
            own = [wide[e : e + 1] for e in range(18)]
            if direction == 0:
                moved = [jnp.where(x_lane == 0, roll(u, 97), roll(u, 1)) for u in own]
            else:
                before = (at + BLOCKS - 1) % BLOCKS
                wide = 0.5 * links[before, direction * 24 : direction * 24 + 24, :].astype(F32)
                other = [wide[e : e + 1] for e in range(18)]
                moved = [
                    jnp.where(lane < LXY, roll(o, LXY), roll(u, LXY)) for o, u in zip(other, own)
                ]
            for e in range(18):
                table[2 * direction, e : e + 1, block(at)] = own[e]
            for e, value in enumerate(minus_adjoint(moved)):
                table[2 * direction + 1, e : e + 1, block(at)] = value


def fill_z_tables(links, links_z, table):
    for at in range(BLOCKS):
        lanes = slice(at * LANES, (at + 1) * LANES)
        if at < BLOCKS // 2:
            wide = 0.5 * links[at, 48:72, :].astype(F32)
            straight, turned = 4, 5
        else:
            wide = 0.5 * links_z[at - BLOCKS // 2, 0:24, :].astype(F32)
            straight, turned = 5, 4
        own = [wide[e : e + 1] for e in range(18)]
        for e in range(18):
            table[straight, e : e + 1, lanes] = own[e]
        for e, value in enumerate(minus_adjoint(own)):
            table[turned, e : e + 1, lanes] = value


def fill_order(core, side, order):
    bits = side.bit_length() - 1
    width = 2 * side * side
    row = lax.broadcasted_iota(jnp.int32, (width, width), 0)
    column = lax.broadcasted_iota(jnp.int32, (width, width), 1)
    low = jnp.bitwise_and(row, side - 1)
    place = jnp.bitwise_and(jnp.right_shift(row, bits), side - 1)
    rest = row - low - place * side
    high = jnp.right_shift(place, 1) + (side // 2) * jnp.bitwise_and(place, 1)
    number = jnp.where(core == 1, low * side + high, high * side + low)
    order[...] = jnp.where(column == rest + number, 1.0, 0.0)


def kernel(
    side, x_ref, links_ref, momenta_ref, directions_ref, out_ref,
    ra, rb, spread, field, field_b, halo, links_z_out, links, links_z, table, cosine, sine, order,
    twisted, twisted_h, packed_xy, packed_z, packed_h, acc_xy, acc_z, send_xy, send_z, got_xy, got_z,
    sum_xy, sum_z, rows_out, rows_in, last,
    ready, sem_a, sem_b, sem_h, sem_l, sem_r, sem_s,
):
    nev = side * side
    pairs = side // 2
    group = 2 * side
    me, core = lax.axis_index("space"), lax.axis_index("tm")
    high, low = me // side, me % side
    a = low + core * (high - low)
    b = high + core * (low - high)

    def device(at_a, at_b):
        return (1 - core) * (at_b * side + at_a) + core * (at_a * side + at_b)

    above = (me + 1) % nev
    below = (me + nev - 1) % nev

    barrier = pltpu.get_barrier_semaphore()

    def greet(target):
        pl.semaphore_signal(barrier, inc=1, device_id={"space": target}, device_id_type=MESH)

    beside_b = (device(a, (b + 1) % side), device(a, (b + side - 1) % side))
    for step in range(1, side):
        greet(device((a + step) % side, b))
    for target in (above, below) + beside_b:
        greet(target)
    pack_links(links_ref, links, links_z_out)
    pl.semaphore_wait(barrier, side - 1 + 4)

    def send(src, dst, sent, arrived, target):
        copy = pltpu.make_async_remote_copy(
            src_ref=src, dst_ref=dst, send_sem=sent, recv_sem=arrived,
            device_id={"space": target}, device_id_type=MESH,
        )
        copy.start()
        return copy

    far_a = sorted(range(1, side), key=lambda k: -min(k, side - k))
    turns = [0] + sorted(range(1, pairs), key=lambda k: -min(k, pairs - k))

    def member_of(turn, member):
        return (b + turn) % pairs + member * pairs

    for step in far_a:
        to_a = (a + step) % side

        @pl.when(core == 0)
        def _():
            send(x_ref.at[:, to_a], ra.at[a], sem_s.at[2], sem_a, device(to_a, b))

        @pl.when(core == 1)
        def _():
            send(x_ref.at[to_a], ra.at[a], sem_s.at[2], sem_a, device(to_a, b))

    links_copy = send(links_z_out, links_z, sem_s.at[1], sem_l, above)
    for to_b in range(side):
        ra[a, to_b] = x_ref[
            (1 - core) * to_b + core * a, (1 - core) * a + core * to_b
        ]
    fill_phases(momenta_ref, me, nev, cosine, sine)
    fill_order(core, side, order)
    fill_tables(links, table)

    for place in range(side // 2 - 1):
        for target in beside_b:
            pl.semaphore_signal(
                ready.at[place], inc=1, device_id={"space": target}, device_id_type=MESH
            )
        pl.semaphore_wait(ready.at[place], 2)

    wait_for(ra.at[pl.ds(0, side - 1)], sem_a)
    for turn in turns:
        for member in range(2 if turn else 1):
            to_b = member_of(turn, member) if turn else (b + pairs) % side
            send(ra.at[:, to_b], rb.at[b], sem_s.at[3], sem_b.at[turn], device(a, to_b))
    for from_a in range(side):
        rb[b, from_a] = ra[from_a, b]

    links_copy.wait()
    fill_z_tables(links, links_z, table)
    upper = pl.ds(HALF, HALF)
    lane = lax.broadcasted_iota(jnp.int32, (1, LANES), 1)
    x_lane = jnp.bitwise_and(lane, LXY - 1)
    lower_half = pl.ds(0, HALF)

    def pair_of(turn):
        return (b + pairs - turn) % pairs

    def own_plane(turn):
        pair = pair_of(turn)
        rows_at = pl.multiple_of(pair * group, group)
        wait_for(rb.at[pl.ds(0, 2 if turn else 1)], sem_b.at[turn])
        for member in range(2):
            for from_a in range(side):
                spread[pl.ds((member * side + from_a) * PITCH, BLOCK_ROWS), :] = rb[
                    pair + member * pairs, from_a
                ].astype(F32)
        for comp in range(COMPS):
            for at in range(BLOCKS):
                rows = spread[pl.ds(comp * BLOCKS + at, group, stride=PITCH), :]
                field[comp, :, at * LANES : (at + 1) * LANES] = rows
                field_b[pair, comp, :, at * LANES : (at + 1) * LANES] = rows.astype(BF16)
        send(
            field_b.at[pair, :, :, lower_half], halo.at[pair, :, :, lower_half],
            sem_s.at[4], sem_h.at[0, pair], below,
        )
        send(
            field_b.at[pair, :, :, upper], halo.at[pair, :, :, upper],
            sem_s.at[4], sem_h.at[1, pair], above,
        )

        @pl.loop(0, BLOCKS)
        def _(at):
            lanes = lanes_at(0, at)
            after = lanes_at(0, (at + 1) % BLOCKS)
            before = lanes_at(0, (at + BLOCKS - 1) % BLOCKS)
            vec = [field[c, :, lanes] for c in range(COMPS)]
            store_twisted(twisted, 0, nev, rows_at, group, at, cosine.at[0], sine.at[0], vec)
            ahead = [jnp.where(x_lane == LXY - 1, roll(v, 31), roll(v, 127)) for v in vec]
            behind = [jnp.where(x_lane == 0, roll(v, 97), roll(v, 1)) for v in vec]
            first = apply_table(table.at[0], lanes, ahead)
            second = apply_table(table.at[1], lanes, behind)
            store_packed(
                packed_xy, 0, 0, nev, rows_at, group, at, [f + s for f, s in zip(first, second)]
            )
            ahead = [
                jnp.where(lane < LANES - LXY, roll(v, 96), roll(field[c, :, after], 96))
                for c, v in enumerate(vec)
            ]
            behind = [
                jnp.where(lane < LXY, roll(field[c, :, before], LXY), roll(v, LXY))
                for c, v in enumerate(vec)
            ]
            first = apply_table(table.at[2], lanes, ahead)
            second = apply_table(table.at[3], lanes, behind)
            store_packed(
                packed_xy, 2 * nev, 0, nev, rows_at, group, at,
                [f + s for f, s in zip(first, second)],
            )
            store_packed(
                packed_h, 0, 0, nev, rows_at, group, at,
                apply_table(table.at[5], lanes, vec),
            )

    def halo_wait(which):
        for turn in which:
            wait_for(halo.at[0, :, :, lower_half], sem_h.at[0, pair_of(turn)])
            wait_for(halo.at[0, :, :, upper], sem_h.at[1, pair_of(turn)])

    def beside_block(turn, at):
        pair = pair_of(turn)
        rows_at = pl.multiple_of(pair * group, group)
        lanes = lanes_at(0, at)
        vec = [halo[pair, c, :, lanes].astype(F32) for c in range(COMPS)]
        store_twisted(twisted_h, 0, nev, rows_at, group, at, cosine.at[1], sine.at[1], vec)
        store_packed(
            packed_z, 0, 0, nev, rows_at, group, at, apply_table(table.at[4], lanes, vec)
        )

    def spread_sums(acc, parts, outgoing, got, sent, sem):
        width = parts * side
        for to_a in range(side):
            for mom in range(NMOM):
                for index in range(parts):
                    at = mom * width + index * side
                    outgoing[to_a, at : at + side, :] = acc[
                        index, pl.ds(mom * nev + to_a, side, stride=side), :
                    ].astype(BF16)
        for step in far_a:
            to_a = (a + step) % side
            send(outgoing.at[to_a], got.at[step - 1], sent, sem, device(to_a, b))

    def collect_sums(outgoing, got, total, sem):
        wait_for(got, sem)
        value = outgoing[a].astype(F32)
        for index in range(side - 1):
            value = value + got[index].astype(F32)
        total[...] = value

    for turn in turns:
        own_plane(turn)
    halo_wait(turns[:-1])
    acc_xy[...] = jnp.zeros_like(acc_xy)

    @pl.loop(0, BLOCKS // 2)
    def _(half):
        total = None
        for slot in range(COMPS):
            part = pl.ds(pl.multiple_of(slot * PLANE + half * 2 * LANES, 2 * LANES), 2 * LANES)
            product = contract(twisted[:, part], packed_xy[:, part])
            total = product if total is None else total + product
        for index in range(2):
            acc_xy[index] += total[:, index * 2 * nev : (index + 1) * 2 * nev]
        for turn in turns[:-1]:
            for at in range(2):
                beside_block(turn, 2 * half + at)

    spread_sums(acc_xy, 2, send_xy, got_xy, sem_s.at[5], sem_r.at[0])
    halo_wait(turns[-1:])

    @pl.loop(0, BLOCKS)
    def _(at):
        beside_block(turns[-1], at)

    acc_z[0] = contract(twisted[...], packed_z[...]) + contract(twisted_h[...], packed_h[...])
    spread_sums(acc_z, 1, send_z, got_z, sem_s.at[6], sem_r.at[1])

    collect_sums(send_xy, got_xy, sum_xy, sem_r.at[0])
    collect_sums(send_z, got_z, sum_z, sem_r.at[1])
    for place in range(side):
        rows_out[place, 0 : 2 * NMOM, :] = sum_xy[pl.ds(place, 2 * NMOM, stride=side), :]
        rows_out[place, 2 * NMOM :, :] = sum_z[pl.ds(place, NMOM, stride=side), :]

    def place_of(at_b):
        return 2 * (at_b % pairs) + at_b // pairs

    for step in far_a:
        to_b = (b + step) % side
        send(rows_out.at[place_of(to_b)], rows_in.at[step - 1], sem_s.at[7], sem_r.at[2], device(a, to_b))
    wait_for(rows_in, sem_r.at[2])
    value = rows_out[place_of(b)]
    for index in range(side - 1):
        value = value + rows_in[index]
    last[...] = jnp.dot(
        value, order[...], preferred_element_type=F32, precision=lax.Precision.HIGHEST
    )
    by_dir = [
        last[pl.ds(0, NMOM, stride=2), :],
        last[pl.ds(1, NMOM, stride=2), :],
        last[2 * NMOM :, :],
    ]
    for slot in range(NDIR):
        chosen = directions_ref[slot]
        out_ref[slot] = jnp.where(
            chosen == 0, by_dir[0], jnp.where(chosen == 1, by_dir[1], by_dir[2])
        )

    wait_for(ra.at[pl.ds(0, side - 1)], sem_s.at[2])
    wait_for(rb.at[pl.ds(0, side - 1)], sem_s.at[3])
    wait_for(field_b, sem_s.at[4])
    wait_for(got_xy, sem_s.at[5])
    wait_for(got_z, sem_s.at[6])
    wait_for(rows_in, sem_s.at[7])


def shards(vectors, gauge_links, momenta, directions):
    space = lax.axis_size("space")
    side = math.isqrt(space)
    nev, pairs, group = space, side // 2, 2 * side
    blocks = vectors.reshape(COMPS, space, BLOCKS, LANES)
    blocks = jnp.transpose(blocks, (1, 0, 2, 3)).reshape(side, side, BLOCK_ROWS, LANES)
    scratch = [
        ((side, side, BLOCK_ROWS, LANES), BF16),
        ((side, side, BLOCK_ROWS, LANES), BF16),
        ((group * PITCH, LANES), F32),
        ((COMPS, group, PLANE), F32),
        ((pairs, COMPS, group, PLANE), BF16),
        ((pairs, COMPS, group, PLANE), BF16),
        ((BLOCKS // 2, 32, LANES), BF16),
        ((BLOCKS, 80, LANES), BF16),
        ((BLOCKS // 2, 32, LANES), BF16),
        ((6, 24, PLANE), F32),
        ((2, NMOM, PLANE), F32),
        ((2, NMOM, PLANE), F32),
        ((2 * nev, 2 * nev), F32),
        ((NMOM * nev, DEPTH), BF16),
        ((NMOM * nev, DEPTH), BF16),
        ((4 * nev, DEPTH), BF16),
        ((2 * nev, DEPTH), BF16),
        ((2 * nev, DEPTH), BF16),
        ((2, NMOM * nev, 2 * nev), F32),
        ((1, NMOM * nev, 2 * nev), F32),
        ((side, 2 * NMOM * side, 2 * nev), BF16),
        ((side, NMOM * side, 2 * nev), BF16),
        ((side - 1, 2 * NMOM * side, 2 * nev), BF16),
        ((side - 1, NMOM * side, 2 * nev), BF16),
        ((2 * NMOM * side, 2 * nev), F32),
        ((NMOM * side, 2 * nev), F32),
        ((side, NDIR * NMOM, 2 * nev), F32),
        ((side - 1, NDIR * NMOM, 2 * nev), F32),
        ((NDIR * NMOM, 2 * nev), F32),
    ]
    dma = pltpu.SemaphoreType.DMA
    out = pl.pallas_call(
        functools.partial(kernel, side),
        out_shape=jax.ShapeDtypeStruct((NDIR, NMOM, 2 * nev), F32),
        in_specs=[
            pl.BlockSpec(memory_space=pltpu.VMEM),
            pl.BlockSpec(memory_space=pltpu.VMEM),
            pl.BlockSpec(memory_space=pltpu.SMEM),
            pl.BlockSpec(memory_space=pltpu.SMEM),
        ],
        out_specs=pl.BlockSpec(memory_space=pltpu.VMEM),
        scratch_shapes=[pltpu.VMEM(*s) for s in scratch]
        + [pltpu.SemaphoreType.REGULAR((max(1, side // 2 - 1),))]
        + [dma, dma((pairs,)), dma((2, pairs)), dma, dma((3,)), dma((8,))],
        compiler_params=pltpu.CompilerParams(
            collective_id=0, has_side_effects=True, vmem_limit_bytes=60 * 1024 * 1024
        ),
    )(blocks, gauge_links[0], momenta.T, directions)
    return jnp.transpose(out, (1, 0, 2))[None, None]


def solution(mesh):
    return jax.shard_map(
        shards,
        mesh=mesh,
        in_specs=(
            P(("cfg", "tm"), "space", None, None),
            P(("cfg", "tm"), None, None, "space"),
            P(),
            P(),
        ),
        out_specs=P("space", ("cfg", "tm"), None, None, None),
        check_vma=False,
    )
```

profile of v0, /device:TPU:514, one launch (start us, length us, event | category | flops | bytes accessed | tf_op | source)
XLA Modules:
  0.0 85.2 jit_solution(11230938252782857187)
XLA Ops:
  0.0 1.3 %copy.8 = bf16[1,6,512,128]{3,2,1,0:T(8,128)(2,1)S(1)} copy(bf16[1,6,512,128]{3,1,2,0:T(8,128)(2,1)} %bitcast.16) | data formatting | bytes 1572864
  1.3 1.0 %copy.5 = bf16[6,64,8,128]{3,2,0,1:T(8,128)(2,1)} copy(bf16[6,64,8,128]{3,2,1,0:T(8,128)(2,1)S(1)} %bitcast.14) | data formatting | bytes 1572864 | tf_op jit(solution)/shard_map/reshape | solution.py:434
  2.3 81.5 %shard_map.46 = f32[3,8,128]{2,1,0:T(8,128)} custom-call(bf16[8,8,48,128]{3,2,1,0:T(8,128)(2,1)} %bitcast.15, bf16[3,18,1024]{2,1,0:T(8,128)(2,1)} %bitcast.17, s32[3,8]{1,0:T(4,128)} %bitcast.19, s32[3]{0:T(128)} %directions_ref.1), custom_call_target="tpu_custom_call" | custom-call | tf_op jit(solution)/shard_map/pallas_call | solution.py:468
  83.9 1.3 %copy.10 = f32[1,1,8,3,128]{4,2,3,1,0:T(8,128)} copy(f32[1,1,8,3,128]{4,2,3,1,0:T(8,128)} %bitcast.18) | data formatting | bytes 24576
where the time goes:
time: 85.4 us; the launch traced here: 85.2 us
  Pallas kernels  81.5 us (95%)
  local copies, waits for them, and re-layouts  3.65 us (4%)
    pallas_call x1, Pallas kernels, shards(): pl.pallas_call(functools.partial(kernel, side), out_shape=jax.ShapeDtypeS...  81.5 us
    unnamed x2, local copies, waits for them, and re-layouts  2.64 us

commit v1 on v0

--- a/solution.py
+++ b/solution.py
@@ -220,10 +220,7 @@
         return copy
 
     far_a = sorted(range(1, side), key=lambda k: -min(k, side - k))
-    turns = [0] + sorted(range(1, pairs), key=lambda k: -min(k, pairs - k))
-
-    def member_of(turn, member):
-        return (b + turn) % pairs + member * pairs
+    own_pair = b % pairs
 
     for step in far_a:
         to_a = (a + step) % side
@@ -253,10 +250,10 @@
         pl.semaphore_wait(ready.at[place], 2)
 
     wait_for(ra.at[pl.ds(0, side - 1)], sem_a)
-    for turn in turns:
+    for turn in reversed(range(pairs)):
         for member in range(2 if turn else 1):
-            to_b = member_of(turn, member) if turn else (b + pairs) % side
-            send(ra.at[:, to_b], rb.at[b], sem_s.at[3], sem_b.at[turn], device(a, to_b))
+            to_b = (b + turn) % pairs + member * pairs if turn else (b + pairs) % side
+            send(ra.at[:, to_b], rb.at[b], sem_s.at[3], sem_b.at[own_pair], device(a, to_b))
     for from_a in range(side):
         rb[b, from_a] = ra[from_a, b]
 
@@ -267,13 +264,16 @@
     x_lane = jnp.bitwise_and(lane, LXY - 1)
     lower_half = pl.ds(0, HALF)
 
-    def pair_of(turn):
-        return (b + pairs - turn) % pairs
-
-    def own_plane(turn):
-        pair = pair_of(turn)
+    def own_plane(pair):
         rows_at = pl.multiple_of(pair * group, group)
-        wait_for(rb.at[pl.ds(0, 2 if turn else 1)], sem_b.at[turn])
+        @pl.when(pair == own_pair)
+        def _():
+            wait_for(rb.at[pl.ds(0, 1)], sem_b.at[pair])
+
+        @pl.when(pair != own_pair)
+        def _():
+            wait_for(rb.at[pl.ds(0, 2)], sem_b.at[pair])
+
         for member in range(2):
             for from_a in range(side):
                 spread[pl.ds((member * side + from_a) * PITCH, BLOCK_ROWS), :] = rb[
@@ -327,13 +327,12 @@
             )
 
     def halo_wait(which):
-        for turn in which:
-            wait_for(halo.at[0, :, :, lower_half], sem_h.at[0, pair_of(turn)])
-            wait_for(halo.at[0, :, :, upper], sem_h.at[1, pair_of(turn)])
-
-    def beside_block(turn, at):
-        pair = pair_of(turn)
-        rows_at = pl.multiple_of(pair * group, group)
+        for pair in which:
+            wait_for(halo.at[0, :, :, lower_half], sem_h.at[0, pair])
+            wait_for(halo.at[0, :, :, upper], sem_h.at[1, pair])
+
+    def beside_block(pair, at):
+        rows_at = pair * group
         lanes = lanes_at(0, at)
         vec = [halo[pair, c, :, lanes].astype(F32) for c in range(COMPS)]
         store_twisted(twisted_h, 0, nev, rows_at, group, at, cosine.at[1], sine.at[1], vec)
@@ -361,9 +360,10 @@
             value = value + got[index].astype(F32)
         total[...] = value
 
-    for turn in turns:
-        own_plane(turn)
-    halo_wait(turns[:-1])
+    for index in range(pairs - 1):
+        own_plane(1 + (index + own_pair) % (pairs - 1))
+    own_plane(0)
+    halo_wait(range(1, pairs))
     acc_xy[...] = jnp.zeros_like(acc_xy)
 
     @pl.loop(0, BLOCKS // 2)
@@ -375,16 +375,16 @@
             total = product if total is None else total + product
         for index in range(2):
             acc_xy[index] += total[:, index * 2 * nev : (index + 1) * 2 * nev]
-        for turn in turns[:-1]:
+        for pair in range(1, pairs):
             for at in range(2):
-                beside_block(turn, 2 * half + at)
+                beside_block(pair, 2 * half + at)
 
     spread_sums(acc_xy, 2, send_xy, got_xy, sem_s.at[5], sem_r.at[0])
-    halo_wait(turns[-1:])
+    halo_wait([0])
 
     @pl.loop(0, BLOCKS)
     def _(at):
-        beside_block(turns[-1], at)
+        beside_block(0, at)
 
     acc_z[0] = contract(twisted[...], packed_z[...]) + contract(twisted_h[...], packed_h[...])
     spread_sums(acc_z, 1, send_z, got_z, sem_s.at[6], sem_r.at[1])

time: 85.4 us -> 77 us (0.902)
  Pallas kernels: 81.5 us -> 73.1 us
    pallas_call x1, Pallas kernels: 81.5 us -> 73.1 us  [shards(): pl.pallas_call(functools.partial(kernel, side), out_shape=jax.ShapeDtypeS...]
where the time goes in v1:
time: 77 us; the launch traced here: 76.8 us
  Pallas kernels  73.1 us (95%)
  local copies, waits for them, and re-layouts  3.65 us (5%)
    pallas_call x1, Pallas kernels, shards(): pl.pallas_call(functools.partial(kernel, side), out_shape=jax.ShapeDtypeS...  73.1 us
    unnamed x2, local copies, waits for them, and re-layouts  2.64 us

profile of v1, /device:TPU:514, one launch (start us, length us, event | category | flops | bytes accessed | tf_op | source)
XLA Modules:
  0.0 76.8 jit_solution(9682014387200839287)
XLA Ops:
  0.0 1.3 %copy.8 = bf16[1,6,512,128]{3,2,1,0:T(8,128)(2,1)S(1)} copy(bf16[1,6,512,128]{3,1,2,0:T(8,128)(2,1)} %bitcast.16) | data formatting | bytes 1572864
  1.3 1.0 %copy.5 = bf16[6,64,8,128]{3,2,0,1:T(8,128)(2,1)} copy(bf16[6,64,8,128]{3,2,1,0:T(8,128)(2,1)S(1)} %bitcast.14) | data formatting | bytes 1572864 | tf_op jit(solution)/shard_map/reshape | solution.py:434
  2.3 73.1 %shard_map.46 = f32[3,8,128]{2,1,0:T(8,128)} custom-call(bf16[8,8,48,128]{3,2,1,0:T(8,128)(2,1)} %bitcast.15, bf16[3,18,1024]{2,1,0:T(8,128)(2,1)} %bitcast.17, s32[3,8]{1,0:T(4,128)} %bitcast.19, s32[3]{0:T(128)} %directions_ref.1), custom_call_target="tpu_custom_call" | custom-call | tf_op jit(solution)/shard_map/pallas_call | solution.py:468
  75.5 1.3 %copy.10 = f32[1,1,8,3,128]{4,2,3,1,0:T(8,128)} copy(f32[1,1,8,3,128]{4,2,3,1,0:T(8,128)} %bitcast.18) | data formatting | bytes 24576

commit v2 on v1

--- a/solution.py
+++ b/solution.py
@@ -65,23 +65,27 @@
         packed[lower, lanes_at(first + 3 + colour, at)] = -re
 
 
-def store_twisted(twisted, first, nev, rows_at, group, at, cosine, sine, field):
+def store_twisted(twisted, pair, group, at, cosine, sine, field):
     for mom in range(NMOM):
         cos_row = cosine[mom : mom + 1, lanes_at(0, at)]
         sin_row = sine[mom : mom + 1, lanes_at(0, at)]
-        rows = pl.ds(mom * nev + rows_at, group)
+        rows = pl.ds(pl.multiple_of(pair * NMOM * group, group) + mom * group, group)
         for colour in range(3):
             vec_re, vec_im = field[colour], field[3 + colour]
-            twisted[rows, lanes_at(first + colour, at)] = (
+            twisted[rows, lanes_at(colour, at)] = (
                 vec_re * cos_row - vec_im * sin_row
             ).astype(BF16)
-            twisted[rows, lanes_at(first + 3 + colour, at)] = (
+            twisted[rows, lanes_at(3 + colour, at)] = (
                 vec_re * sin_row + vec_im * cos_row
             ).astype(BF16)
 
 
 def contract(left, right):
     return lax.dot_general(left, right, (((1,), (1,)), ((), ())), preferred_element_type=F32)
+
+
+def rounds_of(side):
+    return (side - 1).bit_length() if side > 2 else 0
 
 
 def wait_for(ref, sem):
@@ -110,6 +114,25 @@
             theta = TWO_PI * (part_x + part_y + part_z)
             cosine[index, :, at * LANES : (at + 1) * LANES] = jnp.cos(theta)
             sine[index, :, at * LANES : (at + 1) * LANES] = jnp.sin(theta)
+
+
+def make_blocks(side, raw, tiles, blocks):
+    @pl.loop(0, side)
+    def _(high):
+        for low in range(side):
+            start = pl.multiple_of((high * side + low) * PLANE, PLANE)
+            plane = raw[:, pl.ds(start, PLANE)].astype(F32)
+            for at in range(BLOCKS):
+                row = (low * BLOCKS + at) * 8
+                tiles[row : row + COMPS, :] = plane[:, at * LANES : (at + 1) * LANES]
+            for comp in range(0, COMPS, 2):
+                pieces = [
+                    tiles[pl.ds(low * BLOCKS * 8 + c, BLOCKS, stride=8), :]
+                    for c in (comp, comp + 1)
+                ]
+                blocks[high, low, comp * BLOCKS : (comp + 2) * BLOCKS, :] = jnp.concatenate(
+                    pieces, axis=0
+                ).astype(BF16)
 
 
 def pack_links(links_ref, links_out, links_z_out):
@@ -178,11 +201,12 @@
 
 
 def kernel(
-    side, x_ref, links_ref, momenta_ref, directions_ref, out_ref,
+    side, vectors_hbm, links_hbm, momenta_hbm, directions_hbm, out_ref,
+    raw, tiles, x_ref, links_ref, momenta_ref, directions_ref,
     ra, rb, spread, field, field_b, halo, links_z_out, links, links_z, table, cosine, sine, order,
-    twisted, twisted_h, packed_xy, packed_z, packed_h, acc_xy, acc_z, send_xy, send_z, got_xy, got_z,
-    sum_xy, sum_z, rows_out, rows_in, last,
-    ready, sem_a, sem_b, sem_h, sem_l, sem_r, sem_s,
+    twisted, twisted_h, twisted_h0, packed_xy, packed_z, packed_h, acc_xy, acc_z, send_xy, send_z, got_xy, got_z,
+    sum_xy, sum_z, rows_out, rows_in,
+    sem_i, ready, sem_a, sem_b, sem_h, sem_l, sem_r, sem_s,
 ):
     nev = side * side
     pairs = side // 2
@@ -203,13 +227,37 @@
     def greet(target):
         pl.semaphore_signal(barrier, inc=1, device_id={"space": target}, device_id_type=MESH)
 
-    beside_b = (device(a, (b + 1) % side), device(a, (b + side - 1) % side))
+    def has_up(distance):
+        return 1 - (b + distance) // side
+
+    def has_down(distance):
+        return (b + side - distance) // side
+
+    def tell(distance, signal):
+        @pl.when(has_up(distance) == 1)
+        def _():
+            signal(device(a, b + distance))
+
+        @pl.when(has_down(distance) == 1)
+        def _():
+            signal(device(a, b - distance))
+
     for step in range(1, side):
         greet(device((a + step) % side, b))
-    for target in (above, below) + beside_b:
-        greet(target)
+    tell(1, greet)
+    sources = (vectors_hbm, links_hbm, momenta_hbm, directions_hbm)
+    targets = (raw, links_ref, momenta_ref, directions_ref)
+    inputs = [
+        pltpu.make_async_copy(source, target, sem_i.at[index])
+        for index, (source, target) in enumerate(zip(sources, targets))
+    ]
+    for copy in inputs:
+        copy.start()
+    inputs[0].wait()
+    make_blocks(side, raw, tiles, x_ref)
+    inputs[1].wait()
     pack_links(links_ref, links, links_z_out)
-    pl.semaphore_wait(barrier, side - 1 + 4)
+    pl.semaphore_wait(barrier, side - 1 + has_up(1) + has_down(1))
 
     def send(src, dst, sent, arrived, target):
         copy = pltpu.make_async_remote_copy(
@@ -233,21 +281,27 @@
         def _():
             send(x_ref.at[to_a], ra.at[a], sem_s.at[2], sem_a, device(to_a, b))
 
-    links_copy = send(links_z_out, links_z, sem_s.at[1], sem_l, above)
     for to_b in range(side):
         ra[a, to_b] = x_ref[
             (1 - core) * to_b + core * a, (1 - core) * a + core * to_b
         ]
+    inputs[2].wait()
+    inputs[3].wait()
     fill_phases(momenta_ref, me, nev, cosine, sine)
     fill_order(core, side, order)
     fill_tables(links, table)
 
-    for place in range(side // 2 - 1):
-        for target in beside_b:
+    for place in range(rounds_of(side)):
+
+        def mark(target):
             pl.semaphore_signal(
                 ready.at[place], inc=1, device_id={"space": target}, device_id_type=MESH
             )
-        pl.semaphore_wait(ready.at[place], 2)
+
+        tell(2**place, mark)
+        pl.semaphore_wait(ready.at[place], has_up(2**place) + has_down(2**place))
+
+    links_copy = send(links_z_out, links_z, sem_s.at[1], sem_l, above)
 
     wait_for(ra.at[pl.ds(0, side - 1)], sem_a)
     for turn in reversed(range(pairs)):
@@ -264,8 +318,7 @@
     x_lane = jnp.bitwise_and(lane, LXY - 1)
     lower_half = pl.ds(0, HALF)
 
-    def own_plane(pair):
-        rows_at = pl.multiple_of(pair * group, group)
+    def own_arrive(pair):
         @pl.when(pair == own_pair)
         def _():
             wait_for(rb.at[pl.ds(0, 1)], sem_b.at[pair])
@@ -293,61 +346,69 @@
             sem_s.at[4], sem_h.at[1, pair], above,
         )
 
+
+    def own_block(pair, at):
+        rows_at = pl.multiple_of(pair * group, group)
+        lanes = lanes_at(0, at)
+        after = lanes_at(0, (at + 1) % BLOCKS)
+        before = lanes_at(0, (at + BLOCKS - 1) % BLOCKS)
+        vec = [field[c, :, lanes] for c in range(COMPS)]
+        store_twisted(twisted, pair, group, at, cosine.at[0], sine.at[0], vec)
+        ahead = [jnp.where(x_lane == LXY - 1, roll(v, 31), roll(v, 127)) for v in vec]
+        behind = [jnp.where(x_lane == 0, roll(v, 97), roll(v, 1)) for v in vec]
+        first = apply_table(table.at[0], lanes, ahead)
+        second = apply_table(table.at[1], lanes, behind)
+        store_packed(
+            packed_xy, 0, 0, nev, rows_at, group, at, [f + s for f, s in zip(first, second)]
+        )
+        ahead = [
+            jnp.where(lane < LANES - LXY, roll(v, 96), roll(field[c, :, after], 96))
+            for c, v in enumerate(vec)
+        ]
+        behind = [
+            jnp.where(lane < LXY, roll(field[c, :, before], LXY), roll(v, LXY))
+            for c, v in enumerate(vec)
+        ]
+        first = apply_table(table.at[2], lanes, ahead)
+        second = apply_table(table.at[3], lanes, behind)
+        store_packed(
+            packed_xy, 2 * nev, 0, nev, rows_at, group, at,
+            [f + s for f, s in zip(first, second)],
+        )
+        store_packed(
+            packed_h, 0, 0, nev, rows_at, group, at,
+            apply_table(table.at[5], lanes, vec),
+        )
+
+    def own_plane(pair):
+        own_arrive(pair)
+
         @pl.loop(0, BLOCKS)
         def _(at):
-            lanes = lanes_at(0, at)
-            after = lanes_at(0, (at + 1) % BLOCKS)
-            before = lanes_at(0, (at + BLOCKS - 1) % BLOCKS)
-            vec = [field[c, :, lanes] for c in range(COMPS)]
-            store_twisted(twisted, 0, nev, rows_at, group, at, cosine.at[0], sine.at[0], vec)
-            ahead = [jnp.where(x_lane == LXY - 1, roll(v, 31), roll(v, 127)) for v in vec]
-            behind = [jnp.where(x_lane == 0, roll(v, 97), roll(v, 1)) for v in vec]
-            first = apply_table(table.at[0], lanes, ahead)
-            second = apply_table(table.at[1], lanes, behind)
-            store_packed(
-                packed_xy, 0, 0, nev, rows_at, group, at, [f + s for f, s in zip(first, second)]
-            )
-            ahead = [
-                jnp.where(lane < LANES - LXY, roll(v, 96), roll(field[c, :, after], 96))
-                for c, v in enumerate(vec)
-            ]
-            behind = [
-                jnp.where(lane < LXY, roll(field[c, :, before], LXY), roll(v, LXY))
-                for c, v in enumerate(vec)
-            ]
-            first = apply_table(table.at[2], lanes, ahead)
-            second = apply_table(table.at[3], lanes, behind)
-            store_packed(
-                packed_xy, 2 * nev, 0, nev, rows_at, group, at,
-                [f + s for f, s in zip(first, second)],
-            )
-            store_packed(
-                packed_h, 0, 0, nev, rows_at, group, at,
-                apply_table(table.at[5], lanes, vec),
-            )
+            own_block(pair, at)
 
     def halo_wait(which):
         for pair in which:
             wait_for(halo.at[0, :, :, lower_half], sem_h.at[0, pair])
             wait_for(halo.at[0, :, :, upper], sem_h.at[1, pair])
 
-    def beside_block(pair, at):
+    def beside_block(target, place, pair, at):
         rows_at = pair * group
         lanes = lanes_at(0, at)
         vec = [halo[pair, c, :, lanes].astype(F32) for c in range(COMPS)]
-        store_twisted(twisted_h, 0, nev, rows_at, group, at, cosine.at[1], sine.at[1], vec)
+        store_twisted(target, place, group, at, cosine.at[1], sine.at[1], vec)
         store_packed(
             packed_z, 0, 0, nev, rows_at, group, at, apply_table(table.at[4], lanes, vec)
         )
 
     def spread_sums(acc, parts, outgoing, got, sent, sem):
-        width = parts * side
+        width = 2 * NMOM
         for to_a in range(side):
-            for mom in range(NMOM):
-                for index in range(parts):
-                    at = mom * width + index * side
-                    outgoing[to_a, at : at + side, :] = acc[
-                        index, pl.ds(mom * nev + to_a, side, stride=side), :
+            for index in range(parts):
+                for pair in range(pairs):
+                    at = (index * pairs + pair) * width
+                    outgoing[to_a, at : at + width, :] = acc[
+                        index, pl.ds(pair * NMOM * group + to_a, width, stride=side), :
                     ].astype(BF16)
         for step in far_a:
             to_a = (a + step) % side
@@ -365,35 +426,52 @@
     own_plane(0)
     halo_wait(range(1, pairs))
     acc_xy[...] = jnp.zeros_like(acc_xy)
+    acc_z[...] = jnp.zeros_like(acc_z)
+
+    def chunks(half):
+        for slot in range(COMPS):
+            yield pl.ds(pl.multiple_of(slot * PLANE + half * 2 * LANES, 2 * LANES), 2 * LANES)
 
     @pl.loop(0, BLOCKS // 2)
     def _(half):
         total = None
-        for slot in range(COMPS):
-            part = pl.ds(pl.multiple_of(slot * PLANE + half * 2 * LANES, 2 * LANES), 2 * LANES)
+        for part in chunks(half):
             product = contract(twisted[:, part], packed_xy[:, part])
             total = product if total is None else total + product
         for index in range(2):
             acc_xy[index] += total[:, index * 2 * nev : (index + 1) * 2 * nev]
         for pair in range(1, pairs):
             for at in range(2):
-                beside_block(pair, 2 * half + at)
+                beside_block(twisted_h, pair - 1, pair, 2 * half + at)
 
     spread_sums(acc_xy, 2, send_xy, got_xy, sem_s.at[5], sem_r.at[0])
     halo_wait([0])
-
-    @pl.loop(0, BLOCKS)
-    def _(at):
-        beside_block(0, at)
-
-    acc_z[0] = contract(twisted[...], packed_z[...]) + contract(twisted_h[...], packed_h[...])
+    early = slice(NMOM * group, NMOM * nev)
+    late = slice(0, NMOM * group)
+
+    @pl.loop(0, BLOCKS // 2)
+    def _(half):
+        total = None
+        for part in chunks(half):
+            product = contract(twisted_h[:, part], packed_h[:, part])
+            total = product if total is None else total + product
+        acc_z[0, early, :] += total
+        for at in range(2):
+            beside_block(twisted_h0, 0, 0, 2 * half + at)
+
+    acc_z[0, late, :] = contract(twisted_h0[...], packed_h[...])
+    acc_z[0] += contract(twisted[...], packed_z[...])
     spread_sums(acc_z, 1, send_z, got_z, sem_s.at[6], sem_r.at[1])
 
     collect_sums(send_xy, got_xy, sum_xy, sem_r.at[0])
     collect_sums(send_z, got_z, sum_z, sem_r.at[1])
     for place in range(side):
-        rows_out[place, 0 : 2 * NMOM, :] = sum_xy[pl.ds(place, 2 * NMOM, stride=side), :]
-        rows_out[place, 2 * NMOM :, :] = sum_z[pl.ds(place, NMOM, stride=side), :]
+        first = (place // 2) * 2 * NMOM + place % 2
+        for index, total in enumerate((sum_xy, sum_xy, sum_z)):
+            start = first + (index % 2) * NMOM * side
+            rows_out[place, index * NMOM : (index + 1) * NMOM, :] = total[
+                pl.ds(start, NMOM, stride=2), :
+            ]
 
     def place_of(at_b):
         return 2 * (at_b % pairs) + at_b // pairs
@@ -405,14 +483,8 @@
     value = rows_out[place_of(b)]
     for index in range(side - 1):
         value = value + rows_in[index]
-    last[...] = jnp.dot(
-        value, order[...], preferred_element_type=F32, precision=lax.Precision.HIGHEST
-    )
-    by_dir = [
-        last[pl.ds(0, NMOM, stride=2), :],
-        last[pl.ds(1, NMOM, stride=2), :],
-        last[2 * NMOM :, :],
-    ]
+    last = jnp.dot(value, order[...], preferred_element_type=F32, precision=lax.Precision.HIGHEST)
+    by_dir = [last[index * NMOM : (index + 1) * NMOM] for index in range(NDIR)]
     for slot in range(NDIR):
         chosen = directions_ref[slot]
         out_ref[slot] = jnp.where(
@@ -431,9 +503,11 @@
     space = lax.axis_size("space")
     side = math.isqrt(space)
     nev, pairs, group = space, side // 2, 2 * side
-    blocks = vectors.reshape(COMPS, space, BLOCKS, LANES)
-    blocks = jnp.transpose(blocks, (1, 0, 2, 3)).reshape(side, side, BLOCK_ROWS, LANES)
     scratch = [
+        ((COMPS, space * PLANE), BF16),
+        ((side * BLOCKS * 8, LANES), F32),
+        ((side, side, BLOCK_ROWS, LANES), BF16),
+        ((NDIR, 18, PLANE), BF16),
         ((side, side, BLOCK_ROWS, LANES), BF16),
         ((side, side, BLOCK_ROWS, LANES), BF16),
         ((group * PITCH, LANES), F32),
@@ -448,7 +522,8 @@
         ((2, NMOM, PLANE), F32),
         ((2 * nev, 2 * nev), F32),
         ((NMOM * nev, DEPTH), BF16),
-        ((NMOM * nev, DEPTH), BF16),
+        ((NMOM * (nev - group), DEPTH), BF16),
+        ((NMOM * group, DEPTH), BF16),
         ((4 * nev, DEPTH), BF16),
         ((2 * nev, DEPTH), BF16),
         ((2 * nev, DEPTH), BF16),
@@ -462,26 +537,23 @@
         ((NMOM * side, 2 * nev), F32),
         ((side, NDIR * NMOM, 2 * nev), F32),
         ((side - 1, NDIR * NMOM, 2 * nev), F32),
-        ((NDIR * NMOM, 2 * nev), F32),
     ]
     dma = pltpu.SemaphoreType.DMA
     out = pl.pallas_call(
         functools.partial(kernel, side),
         out_shape=jax.ShapeDtypeStruct((NDIR, NMOM, 2 * nev), F32),
-        in_specs=[
-            pl.BlockSpec(memory_space=pltpu.VMEM),
-            pl.BlockSpec(memory_space=pltpu.VMEM),
-            pl.BlockSpec(memory_space=pltpu.SMEM),
-            pl.BlockSpec(memory_space=pltpu.SMEM),
-        ],
+        in_specs=[pl.BlockSpec(memory_space=pl.ANY)] * 4,
         out_specs=pl.BlockSpec(memory_space=pltpu.VMEM),
-        scratch_shapes=[pltpu.VMEM(*s) for s in scratch]
-        + [pltpu.SemaphoreType.REGULAR((max(1, side // 2 - 1),))]
+        scratch_shapes=[pltpu.VMEM(*s) for s in scratch[:4]]
+        + [pltpu.SMEM((NDIR, NMOM), jnp.int32), pltpu.SMEM((NDIR,), jnp.int32)]
+        + [pltpu.VMEM(*s) for s in scratch[4:]]
+        + [dma((4,))]
+        + [pltpu.SemaphoreType.REGULAR((max(1, rounds_of(side)),))]
         + [dma, dma((pairs,)), dma((2, pairs)), dma, dma((3,)), dma((8,))],
         compiler_params=pltpu.CompilerParams(
             collective_id=0, has_side_effects=True, vmem_limit_bytes=60 * 1024 * 1024
         ),
-    )(blocks, gauge_links[0], momenta.T, directions)
+    )(vectors[0, 0], gauge_links[0], momenta.T, directions)
     return jnp.transpose(out, (1, 0, 2))[None, None]
 
 

time: 77 us -> 78.2 us (1.016)
  Pallas kernels: 73.1 us -> 76.7 us
  local copies, waits for them, and re-layouts: 3.65 us -> 1.31 us
    pallas_call x1, Pallas kernels: 73.1 us -> 76.7 us  [shards(): pl.pallas_call(functools.partial(kernel, side), out_shape=jax.ShapeDtypeS...]
    unnamed x2 -> x1, local copies, waits for them, and re-layouts: 2.64 us -> 1.31 us
    reshape x1 -> x0, local copies, waits for them, and re-layouts: 1.01 us -> none  [shards(): blocks = vectors.reshape(COMPS, space, BLOCKS, LANES)]
where the time goes in v2:
time: 78.2 us; the launch traced here: 78 us
  Pallas kernels  76.7 us (98%)
  local copies, waits for them, and re-layouts  1.31 us (2%)
    pallas_call x1, Pallas kernels, shards(): pl.pallas_call(functools.partial(kernel, side), out_shape=jax.ShapeDtypeS...  76.7 us

profile of v2, /device:TPU:514, one launch (start us, length us, event | category | flops | bytes accessed | tf_op | source)
XLA Modules:
  0.0 78.0 jit_solution(12466730789910739162)
XLA Ops:
  0.0 76.7 %shard_map.46 = f32[3,8,128]{2,1,0:T(8,128)} custom-call(bf16[6,65536]{1,0:T(8,128)(2,1)} %bitcast.6, bf16[3,18,1024]{2,1,0:T(8,128)(2,1)} %bitcast.7, s32[3,8]{1,0:T(4,128)} %bitcast.9, s32[3]{0:T(128)} %directions_hbm.1), custom_call_target="tpu_custom_call" | custom-call | tf_op jit(solution)/shard_map/pallas_call | solution.py:542
  76.7 1.3 %copy.6 = f32[1,1,8,3,128]{4,2,3,1,0:T(8,128)} copy(f32[1,1,8,3,128]{4,2,3,1,0:T(8,128)} %bitcast.8) | data formatting | bytes 24576

commit v3 on v2

--- a/solution.py
+++ b/solution.py
@@ -82,10 +82,6 @@
 
 def contract(left, right):
     return lax.dot_general(left, right, (((1,), (1,)), ((), ())), preferred_element_type=F32)
-
-
-def rounds_of(side):
-    return (side - 1).bit_length() if side > 2 else 0
 
 
 def wait_for(ref, sem):
@@ -227,24 +223,11 @@
     def greet(target):
         pl.semaphore_signal(barrier, inc=1, device_id={"space": target}, device_id_type=MESH)
 
-    def has_up(distance):
-        return 1 - (b + distance) // side
-
-    def has_down(distance):
-        return (b + side - distance) // side
-
-    def tell(distance, signal):
-        @pl.when(has_up(distance) == 1)
-        def _():
-            signal(device(a, b + distance))
-
-        @pl.when(has_down(distance) == 1)
-        def _():
-            signal(device(a, b - distance))
-
+    beside_b = (device(a, (b + 1) % side), device(a, (b + side - 1) % side))
     for step in range(1, side):
         greet(device((a + step) % side, b))
-    tell(1, greet)
+    for target in (above, below) + beside_b:
+        greet(target)
     sources = (vectors_hbm, links_hbm, momenta_hbm, directions_hbm)
     targets = (raw, links_ref, momenta_ref, directions_ref)
     inputs = [
@@ -257,7 +240,7 @@
     make_blocks(side, raw, tiles, x_ref)
     inputs[1].wait()
     pack_links(links_ref, links, links_z_out)
-    pl.semaphore_wait(barrier, side - 1 + has_up(1) + has_down(1))
+    pl.semaphore_wait(barrier, side - 1 + 4)
 
     def send(src, dst, sent, arrived, target):
         copy = pltpu.make_async_remote_copy(
@@ -281,6 +264,7 @@
         def _():
             send(x_ref.at[to_a], ra.at[a], sem_s.at[2], sem_a, device(to_a, b))
 
+    links_copy = send(links_z_out, links_z, sem_s.at[1], sem_l, above)
     for to_b in range(side):
         ra[a, to_b] = x_ref[
             (1 - core) * to_b + core * a, (1 - core) * a + core * to_b
@@ -291,17 +275,12 @@
     fill_order(core, side, order)
     fill_tables(links, table)
 
-    for place in range(rounds_of(side)):
-
-        def mark(target):
+    for place in range(side // 2 - 1):
+        for target in beside_b:
             pl.semaphore_signal(
                 ready.at[place], inc=1, device_id={"space": target}, device_id_type=MESH
             )
-
-        tell(2**place, mark)
-        pl.semaphore_wait(ready.at[place], has_up(2**place) + has_down(2**place))
-
-    links_copy = send(links_z_out, links_z, sem_s.at[1], sem_l, above)
+        pl.semaphore_wait(ready.at[place], 2)
 
     wait_for(ra.at[pl.ds(0, side - 1)], sem_a)
     for turn in reversed(range(pairs)):
@@ -548,7 +527,7 @@
         + [pltpu.SMEM((NDIR, NMOM), jnp.int32), pltpu.SMEM((NDIR,), jnp.int32)]
         + [pltpu.VMEM(*s) for s in scratch[4:]]
         + [dma((4,))]
-        + [pltpu.SemaphoreType.REGULAR((max(1, rounds_of(side)),))]
+        + [pltpu.SemaphoreType.REGULAR((max(1, side // 2 - 1),))]
         + [dma, dma((pairs,)), dma((2, pairs)), dma, dma((3,)), dma((8,))],
         compiler_params=pltpu.CompilerParams(
             collective_id=0, has_side_effects=True, vmem_limit_bytes=60 * 1024 * 1024

time: 78.2 us -> 73.9 us (0.945)
  Pallas kernels: 76.7 us -> 72.4 us
    pallas_call x1, Pallas kernels: 76.7 us -> 72.4 us  [shards(): pl.pallas_call(functools.partial(kernel, side), out_shape=jax.ShapeDtypeS...]
where the time goes in v3:
time: 73.9 us; the launch traced here: 73.7 us
  Pallas kernels  72.4 us (98%)
  local copies, waits for them, and re-layouts  1.31 us (2%)
    pallas_call x1, Pallas kernels, shards(): pl.pallas_call(functools.partial(kernel, side), out_shape=jax.ShapeDtypeS...  72.4 us

profile of v3, /device:TPU:514, one launch (start us, length us, event | category | flops | bytes accessed | tf_op | source)
XLA Modules:
  0.0 73.7 jit_solution(16056002935459111037)
XLA Ops:
  0.0 72.4 %shard_map.46 = f32[3,8,128]{2,1,0:T(8,128)} custom-call(bf16[6,65536]{1,0:T(8,128)(2,1)} %bitcast.6, bf16[3,18,1024]{2,1,0:T(8,128)(2,1)} %bitcast.7, s32[3,8]{1,0:T(4,128)} %bitcast.9, s32[3]{0:T(128)} %directions_hbm.1), custom_call_target="tpu_custom_call" | custom-call | tf_op jit(solution)/shard_map/pallas_call | solution.py:521
  72.4 1.3 %copy.6 = f32[1,1,8,3,128]{4,2,3,1,0:T(8,128)} copy(f32[1,1,8,3,128]{4,2,3,1,0:T(8,128)} %bitcast.8) | data formatting | bytes 24576

commit v4 on v3

--- a/solution.py
+++ b/solution.py
@@ -403,40 +403,26 @@
     for index in range(pairs - 1):
         own_plane(1 + (index + own_pair) % (pairs - 1))
     own_plane(0)
+
+    product = contract(twisted[...], packed_xy[...])
+    for index in range(2):
+        acc_xy[index] = product[:, index * 2 * nev : (index + 1) * 2 * nev]
     halo_wait(range(1, pairs))
-    acc_xy[...] = jnp.zeros_like(acc_xy)
-    acc_z[...] = jnp.zeros_like(acc_z)
-
-    def chunks(half):
-        for slot in range(COMPS):
-            yield pl.ds(pl.multiple_of(slot * PLANE + half * 2 * LANES, 2 * LANES), 2 * LANES)
-
-    @pl.loop(0, BLOCKS // 2)
-    def _(half):
-        total = None
-        for part in chunks(half):
-            product = contract(twisted[:, part], packed_xy[:, part])
-            total = product if total is None else total + product
-        for index in range(2):
-            acc_xy[index] += total[:, index * 2 * nev : (index + 1) * 2 * nev]
+
+    @pl.loop(0, BLOCKS)
+    def _(at):
         for pair in range(1, pairs):
-            for at in range(2):
-                beside_block(twisted_h, pair - 1, pair, 2 * half + at)
+            beside_block(twisted_h, pair - 1, pair, at)
 
     spread_sums(acc_xy, 2, send_xy, got_xy, sem_s.at[5], sem_r.at[0])
-    halo_wait([0])
     early = slice(NMOM * group, NMOM * nev)
     late = slice(0, NMOM * group)
-
-    @pl.loop(0, BLOCKS // 2)
-    def _(half):
-        total = None
-        for part in chunks(half):
-            product = contract(twisted_h[:, part], packed_h[:, part])
-            total = product if total is None else total + product
-        acc_z[0, early, :] += total
-        for at in range(2):
-            beside_block(twisted_h0, 0, 0, 2 * half + at)
+    acc_z[0, early, :] = contract(twisted_h[...], packed_h[...])
+    halo_wait([0])
+
+    @pl.loop(0, BLOCKS)
+    def _(at):
+        beside_block(twisted_h0, 0, 0, at)
 
     acc_z[0, late, :] = contract(twisted_h0[...], packed_h[...])
     acc_z[0] += contract(twisted[...], packed_z[...])

time: 73.9 us -> 76.7 us (1.038)
  Pallas kernels: 72.4 us -> 75.2 us
    pallas_call x1, Pallas kernels: 72.4 us -> 75.2 us  [shards(): pl.pallas_call(functools.partial(kernel, side), out_shape=jax.ShapeDtypeS...]
where the time goes in v4:
time: 76.7 us; the launch traced here: 76.5 us
  Pallas kernels  75.2 us (98%)
  local copies, waits for them, and re-layouts  1.31 us (2%)
    pallas_call x1, Pallas kernels, shards(): pl.pallas_call(functools.partial(kernel, side), out_shape=jax.ShapeDtypeS...  75.2 us

profile of v4, /device:TPU:514, one launch (start us, length us, event | category | flops | bytes accessed | tf_op | source)
XLA Modules:
  0.0 76.5 jit_solution(2623053150722557297)
XLA Ops:
  0.0 75.2 %shard_map.46 = f32[3,8,128]{2,1,0:T(8,128)} custom-call(bf16[6,65536]{1,0:T(8,128)(2,1)} %bitcast.6, bf16[3,18,1024]{2,1,0:T(8,128)(2,1)} %bitcast.7, s32[3,8]{1,0:T(4,128)} %bitcast.9, s32[3]{0:T(128)} %directions_hbm.1), custom_call_target="tpu_custom_call" | custom-call | tf_op jit(solution)/shard_map/pallas_call | solution.py:507
  75.2 1.3 %copy.6 = f32[1,1,8,3,128]{4,2,3,1,0:T(8,128)} copy(f32[1,1,8,3,128]{4,2,3,1,0:T(8,128)} %bitcast.8) | data formatting | bytes 24576

commit v5 on v3

--- a/solution.py
+++ b/solution.py
@@ -405,7 +405,6 @@
     own_plane(0)
     halo_wait(range(1, pairs))
     acc_xy[...] = jnp.zeros_like(acc_xy)
-    acc_z[...] = jnp.zeros_like(acc_z)
 
     def chunks(half):
         for slot in range(COMPS):
@@ -424,19 +423,14 @@
                 beside_block(twisted_h, pair - 1, pair, 2 * half + at)
 
     spread_sums(acc_xy, 2, send_xy, got_xy, sem_s.at[5], sem_r.at[0])
-    halo_wait([0])
     early = slice(NMOM * group, NMOM * nev)
     late = slice(0, NMOM * group)
-
-    @pl.loop(0, BLOCKS // 2)
-    def _(half):
-        total = None
-        for part in chunks(half):
-            product = contract(twisted_h[:, part], packed_h[:, part])
-            total = product if total is None else total + product
-        acc_z[0, early, :] += total
-        for at in range(2):
-            beside_block(twisted_h0, 0, 0, 2 * half + at)
+    acc_z[0, early, :] = contract(twisted_h[...], packed_h[...])
+    halo_wait([0])
+
+    @pl.loop(0, BLOCKS)
+    def _(at):
+        beside_block(twisted_h0, 0, 0, at)
 
     acc_z[0, late, :] = contract(twisted_h0[...], packed_h[...])
     acc_z[0] += contract(twisted[...], packed_z[...])

time: 73.9 us -> 76 us (1.028)
  Pallas kernels: 72.4 us -> 74.5 us
    pallas_call x1, Pallas kernels: 72.4 us -> 74.5 us  [shards(): pl.pallas_call(functools.partial(kernel, side), out_shape=jax.ShapeDtypeS...]
where the time goes in v5:
time: 76 us; the launch traced here: 75.8 us
  Pallas kernels  74.5 us (98%)
  local copies, waits for them, and re-layouts  1.31 us (2%)
    pallas_call x1, Pallas kernels, shards(): pl.pallas_call(functools.partial(kernel, side), out_shape=jax.ShapeDtypeS...  74.5 us

profile of v5, /device:TPU:514, one launch (start us, length us, event | category | flops | bytes accessed | tf_op | source)
XLA Modules:
  0.0 75.8 jit_solution(6083823177435270834)
XLA Ops:
  0.0 74.5 %shard_map.46 = f32[3,8,128]{2,1,0:T(8,128)} custom-call(bf16[6,65536]{1,0:T(8,128)(2,1)} %bitcast.6, bf16[3,18,1024]{2,1,0:T(8,128)(2,1)} %bitcast.7, s32[3,8]{1,0:T(4,128)} %bitcast.9, s32[3]{0:T(128)} %directions_hbm.1), custom_call_target="tpu_custom_call" | custom-call | tf_op jit(solution)/shard_map/pallas_call | solution.py:515
  74.5 1.3 %copy.6 = f32[1,1,8,3,128]{4,2,3,1,0:T(8,128)} copy(f32[1,1,8,3,128]{4,2,3,1,0:T(8,128)} %bitcast.8) | data formatting | bytes 24576
